TPU v7x, 256 devices: a whole 4x4x8 slice. The times are simulated.
256 devices in a mesh: head: 2 (over core), outer: 16 (over x, y), inner: 8 (over z).
Axes of the slice: x: 4, y: 4, z: 8, core: 2. Of those that a mesh axis runs over, the one named last changes fastest.
Arguments:
- queries: bfloat16 [65536, 2048], P(('outer', 'inner'), 'head'), may hold values from -6 to 6
- key_rows: bfloat16 [65536, 2048], P(('outer', 'inner'), 'head'), may hold values from -6 to 6
- value_rows: bfloat16 [65536, 2048], P(('outer', 'inner'), 'head'), may hold values from -6 to 6
- teacher_out: bfloat16 [65536, 2048], P(('outer', 'inner'), 'head'), may hold values from -6 to 6
- level_weights: bfloat16 [8, 65536], P(None, ('outer', 'inner')), may hold values from 0.125 to 1
Outputs:
- grad_queries: bfloat16 [65536, 2048], P(('outer', 'inner'), 'head')
- grad_keys: bfloat16 [65536, 2048], P(('outer', 'inner'), 'head')
- grad_values: bfloat16 [65536, 2048], P(('outer', 'inner'), 'head')
- grad_levels: float32 [8, 65536], P(None, ('outer', 'inner'))
All inputs are finite; a program needn't handle non-finite values.
Results may differ from a plain program's by a relative error of at most 0.014.
Values may be sent and summed in bfloat16 or wider, within the bound.
A program may use at most 128 MiB of HBM per device.

v0:
```python
import jax
import jax.numpy as jnp
from jax import lax
from jax.sharding import PartitionSpec as P

DK = 128
LEVELS = 8


def partner_2(value, axis, distance):
    mask = 2**distance
    pairs = [(source, source ^ mask) for source in range(lax.axis_size(axis))]
    return lax.ppermute(value, axis, pairs)


def in_blocks(shard, dim, peers):
    lengths = shard.shape
    parts = shard.reshape(*lengths[:dim], peers, lengths[dim] // peers, *lengths[dim + 1 :])
    return jnp.moveaxis(parts, dim, 0)


def sent_and_summed(shard, axis, dim):
    parts = in_blocks(shard, dim, lax.axis_size(axis))
    arrived = lax.all_to_all(parts, axis, split_axis=0, concat_axis=0, tiled=True)
    return arrived.astype(jnp.float32).sum(axis=0)


def laid_out(parts, dim):
    lengths = list(parts.shape[1:])
    lengths[dim] *= parts.shape[0]
    return jnp.moveaxis(parts, 0, dim).reshape(lengths)


def copy_for_each(shard, axis):
    peers = lax.axis_size(axis)
    return lax.all_to_all(
        jnp.broadcast_to(shard[None], (peers, *shard.shape)), axis, 0, 0, tiled=True
    )


def gathered_copies(shard, axis, dim):
    return laid_out(copy_for_each(shard, axis), dim)


def bit_of(number, position):
    return (number >> position) % 2


def on_device(queries, key_rows, value_rows, teacher_out, level_weights):
    rows_here = queries.shape[0]
    heads_here = queries.shape[1] // DK
    inner_count = lax.axis_size("inner")
    outer_count = lax.axis_size("outer")
    inner_bits = inner_count.bit_length() - 1
    outer_bits = outer_count.bit_length() - 1
    inner_pos = lax.axis_index("inner")
    group_pos = lax.axis_index("outer")
    block_id = group_pos * inner_count + inner_pos
    upper = LEVELS - 1
    gamma = DK ** (-0.5)
    scale_list = [rows_here ** (-0.5)] + [
        gamma * (rows_here * 2 ** (num - 1)) ** (-0.5) for num in range(1, LEVELS)
    ]
    scales = jnp.array(scale_list, dtype=jnp.float32)
    query3 = queries.reshape(rows_here, heads_here, DK)
    key3 = key_rows.reshape(rows_here, heads_here, DK)
    value3 = value_rows.reshape(rows_here, heads_here, DK)
    teacher3 = teacher_out.reshape(rows_here, heads_here, DK)
    block_state = jnp.einsum(
        "thd,the->hde", key3, value3, preferred_element_type=jnp.float32
    ).astype(jnp.bfloat16)
    running = block_state.astype(jnp.float32)
    inner_list = []
    for bit_pos in range(inner_bits):
        partner = partner_2(running.astype(jnp.bfloat16), "inner", bit_pos).astype(running.dtype)
        inner_list.append(jnp.where(bit_of(inner_pos, bit_pos) == 1, partner, 0.0))
        running = running + partner
    inner_levels = jnp.stack(inner_list)
    group_total = running
    group_state = group_total.astype(jnp.bfloat16)
    running = group_state.astype(jnp.float32)
    outer_list = []
    for bit_pos in range(outer_bits):
        partner = partner_2(running.astype(jnp.bfloat16), "outer", bit_pos).astype(running.dtype)
        outer_list.append(jnp.where(bit_of(group_pos, bit_pos) == 1, partner, 0.0))
        running = running + partner
    outer_levels = jnp.stack(outer_list)
    padding = jnp.zeros((upper - inner_bits - outer_bits, heads_here, DK, DK), jnp.float32)
    state_low = jnp.concatenate([inner_levels, outer_levels, padding], axis=0).astype(jnp.bfloat16)
    coefs = level_weights.astype(jnp.float32) * scales[:, None]
    positions = jnp.arange(rows_here, dtype=jnp.int32)
    lower = positions[:, None] >= positions[None, :]
    scores = gamma * jnp.einsum("thd,shd->hts", query3, key3, preferred_element_type=jnp.float32)
    intra_scores = jnp.where(lower[None], scores, 0.0).astype(jnp.bfloat16)
    intra = jnp.einsum("hts,she->the", intra_scores, value3, preferred_element_type=jnp.float32)
    reads = jnp.einsum("thd,lhde->lthe", query3, state_low, preferred_element_type=jnp.float32)
    student = coefs[0][:, None, None] * intra + jnp.sum(coefs[1:, :, None, None] * reads, axis=0)
    error = (student - teacher3.astype(jnp.float32)).astype(jnp.bfloat16)
    error32 = error.astype(jnp.float32)
    back_reads = jnp.einsum("the,lhde->lthd", error, state_low, preferred_element_type=jnp.float32)
    grad_first = scales[0] * jnp.sum(error32 * intra, axis=(1, 2))
    grad_rest = scales[1:, None] * jnp.sum(
        query3.astype(jnp.float32)[None] * back_reads, axis=(2, 3)
    )
    local_grad = jnp.concatenate([grad_first[None], grad_rest], axis=0)
    grad_levels = lax.psum(local_grad, "head")
    intra_error = (coefs[0][:, None, None] * error32).astype(jnp.bfloat16)
    score_raw = gamma * jnp.einsum(
        "the,she->hts", intra_error, value3, preferred_element_type=jnp.float32
    )
    score_grad = jnp.where(lower[None], score_raw, 0.0).astype(jnp.bfloat16)
    grad_query = jnp.einsum(
        "hts,shd->thd", score_grad, key3, preferred_element_type=jnp.float32
    ) + jnp.sum(coefs[1:, :, None, None] * back_reads, axis=0)
    exists = bit_of(block_id, jnp.arange(upper, dtype=jnp.int32)).astype(jnp.float32)
    weighted = ((coefs[1:] * exists[:, None])[:, :, None, None] * error32[None]).astype(
        jnp.bfloat16
    )
    adjoint = jnp.einsum("thd,lthe->lhde", query3, weighted, preferred_element_type=jnp.float32)
    carried = adjoint[:inner_bits]
    inner_adj = jnp.zeros((heads_here, DK, DK), jnp.float32)
    for bit_pos in range(inner_bits):
        partner = partner_2(carried.astype(jnp.bfloat16), "inner", bit_pos).astype(carried.dtype)
        inner_adj = inner_adj + jnp.where(bit_of(inner_pos, bit_pos) == 0, partner[0], 0.0)
        carried = carried[1:] + partner[1:]
    outer_stack = adjoint[inner_bits : inner_bits + outer_bits]
    group_rows = sent_and_summed(outer_stack.astype(jnp.bfloat16), "inner", 2)
    outer_rows = jnp.zeros(group_rows.shape[1:], jnp.float32)
    for bit_pos in range(outer_bits):
        partner = partner_2(group_rows.astype(jnp.bfloat16), "outer", bit_pos).astype(
            group_rows.dtype
        )
        outer_rows = outer_rows + jnp.where(bit_of(group_pos, bit_pos) == 0, partner[0], 0.0)
        group_rows = group_rows[1:] + partner[1:]
    outer_adj = gathered_copies(outer_rows.astype(jnp.bfloat16), "inner", 1).astype(
        outer_rows.dtype
    )
    block_adjoint = (inner_adj + outer_adj).astype(jnp.bfloat16)
    grad_key = jnp.einsum(
        "hts,thd->shd", score_grad, query3, preferred_element_type=jnp.float32
    ) + jnp.einsum("hde,she->shd", block_adjoint, value3, preferred_element_type=jnp.float32)
    grad_value = jnp.einsum(
        "hts,the->she", intra_scores, intra_error, preferred_element_type=jnp.float32
    ) + jnp.einsum("hde,shd->she", block_adjoint, key3, preferred_element_type=jnp.float32)
    width = heads_here * DK
    grad_queries = grad_query.astype(jnp.bfloat16).reshape(rows_here, width)
    grad_keys = grad_key.astype(jnp.bfloat16).reshape(rows_here, width)
    grad_values = grad_value.astype(jnp.bfloat16).reshape(rows_here, width)
    return (grad_queries, grad_keys, grad_values, grad_levels)


def solution(mesh):
    placed = (
        P(("outer", "inner"), "head"),
        P(("outer", "inner"), "head"),
        P(("outer", "inner"), "head"),
        P(("outer", "inner"), "head"),
        P(None, ("outer", "inner")),
    )
    return jax.shard_map(
        on_device,
        mesh=mesh,
        in_specs=placed,
        out_specs=(
            P(("outer", "inner"), "head"),
            P(("outer", "inner"), "head"),
            P(("outer", "inner"), "head"),
            P(None, ("outer", "inner")),
        ),
        check_vma=False,
    )
```

profile of v0, /device:TPU:30, one launch (start us, length us, event | category | flops | bytes accessed | tf_op | source)
XLA Modules:
  0.0 201.3 jit_solution(17561058411118353649)
XLA Ops:
  0.6 1.6 copy.76
  3.4 2.0 collective-permute-start
  5.4 6.3 %collective-permute-done = bf16[8,128,128]{2,1,0:T(8,128)(2,1)S(1)} collective-permute-done((bf16[8,128,128]{2,1,0:T(8,128)(2,1)S(1)}, bf16[8,128,128]{2,1,0:T(8,128)(2,1)S(1)}, u32[]{:S(2)}, u32[]{:S(2)}) %collective-permute-start) | collective-permute-done | bytes 262176 | tf_op jit(solution)/shard_map/ppermute | solution.py:13
  12.5 3.3 %collective-permute-start.1 = (bf16[8,128,128]{2,1,0:T(8,128)(2,1)}, bf16[8,128,128]{2,1,0:T(8,128)(2,1)}, u32[]{:S(2)}, u32[]{:S(2)}) collective-permute-start(bf16[8,128,128]{2,1,0:T(8,128)(2,1)} %fusion.44), channel_id=1, source_target_pairs={{0,2},{1,3},{2,0},{3,1},{4,6},{5,7},{6,4},{7,5},{8,10},{9,11},{10,... | collective-permute-start | bytes 786440 | tf_op jit(solution)/shard_map/ppermute | solution.py:13
  16.8 10.5 %collective-permute-done.1 = bf16[8,128,128]{2,1,0:T(8,128)(2,1)} collective-permute-done((bf16[8,128,128]{2,1,0:T(8,128)(2,1)}, bf16[8,128,128]{2,1,0:T(8,128)(2,1)}, u32[]{:S(2)}, u32[]{:S(2)}) %collective-permute-start.1) | collective-permute-done | bytes 262176 | tf_op jit(solution)/shard_map/ppermute | solution.py:13
  27.3 1.8 fusion.46
  29.2 6.2 %collective-permute-start.2 = (bf16[8,128,128]{2,1,0:T(8,128)(2,1)}, bf16[8,128,128]{2,1,0:T(8,128)(2,1)}, u32[]{:S(2)}, u32[]{:S(2)}) collective-permute-start(bf16[8,128,128]{2,1,0:T(8,128)(2,1)} %fusion.46), channel_id=1, source_target_pairs={{0,4},{1,5},{2,6},{3,7},{4,0},{5,1},{6,2},{7,3},{8,12},{9,13},{10,... | collective-permute-start | bytes 786440 | tf_op jit(solution)/shard_map/ppermute | solution.py:13
  35.4 4.7 %select_convert_fusion.1 = bf16[8,512,512]{2,1,0:T(8,128)(2,1)} fusion(pred[512,512]{1,0:T(8,128)(4,1)S(1)} %iota_compare_fusion, bf16[512,8,128]{0,2,1:T(8,128)(2,1)S(1)} %copy.46, bf16[512,1024]{1,0:T(8,128)(2,1)} %param.7), kind=kOutput, calls=%fused_computation.7 | convolution fusion | flops 543162368 | bytes 6553600 | tf_op jit(solution)/shard_map/thd,shd->hts/dot_general | solution.py:93
  40.2 7.2 %collective-permute-done.2 = bf16[8,128,128]{2,1,0:T(8,128)(2,1)} collective-permute-done((bf16[8,128,128]{2,1,0:T(8,128)(2,1)}, bf16[8,128,128]{2,1,0:T(8,128)(2,1)}, u32[]{:S(2)}, u32[]{:S(2)}) %collective-permute-start.2) | collective-permute-done | bytes 262176 | tf_op jit(solution)/shard_map/ppermute | solution.py:13
  47.4 2.0 fusion.33
  50.1 1.5 copy.63
  51.5 2.6 %copy.40 = f32[512,1024]{0,1:T(8,128)} copy(bf16[512,1024]{1,0:T(8,128)(2,1)} %param.9) | data formatting | bytes 3145728 | tf_op jit(solution)/shard_map/convert_element_type | solution.py:98
  54.2 3.7 %collective-permute-done.3 = bf16[8,128,128]{2,1,0:T(8,128)(2,1)} collective-permute-done((bf16[8,128,128]{2,1,0:T(8,128)(2,1)}, bf16[8,128,128]{2,1,0:T(8,128)(2,1)}, u32[]{:S(2)}, u32[]{:S(2)}) %collective-permute-start.3) | collective-permute-done | bytes 262176 | tf_op jit(solution)/shard_map/ppermute | solution.py:13
  60.2 6.7 %collective-permute-done.4 = bf16[8,128,128]{2,1,0:T(8,128)(2,1)S(1)} collective-permute-done((bf16[8,128,128]{2,1,0:T(8,128)(2,1)S(1)}, bf16[8,128,128]{2,1,0:T(8,128)(2,1)S(1)}, u32[]{:S(2)}, u32[]{:S(2)}) %collective-permute-start.4) | collective-permute-done | bytes 262176 | tf_op jit(solution)/shard_map/ppermute | solution.py:13
  71.3 3.5 %collective-permute-done.5 = bf16[8,128,128]{2,1,0:T(8,128)(2,1)S(1)} collective-permute-done((bf16[8,128,128]{2,1,0:T(8,128)(2,1)S(1)}, bf16[8,128,128]{2,1,0:T(8,128)(2,1)S(1)}, u32[]{:S(2)}, u32[]{:S(2)}) %collective-permute-start.5) | collective-permute-done | bytes 262176 | tf_op jit(solution)/shard_map/ppermute | solution.py:13
  75.9 3.9 %collective-permute-start.6 = (bf16[8,128,128]{2,1,0:T(8,128)(2,1)S(1)}, bf16[8,128,128]{2,1,0:T(8,128)(2,1)S(1)}, u32[]{:S(2)}, u32[]{:S(2)}) collective-permute-start(bf16[8,128,128]{2,1,0:T(8,128)(2,1)S(1)} %fusion.37), channel_id=1, source_target_pairs={{0,64},{8,72},{16,80},{24,88},{32,96},{40,104},{48,112},{56,120},{... | collective-permute-start | bytes 786440 | tf_op jit(solution)/shard_map/ppermute | solution.py:13
  80.0 4.1 %collective-permute-done.6 = bf16[8,128,128]{2,1,0:T(8,128)(2,1)S(1)} collective-permute-done((bf16[8,128,128]{2,1,0:T(8,128)(2,1)S(1)}, bf16[8,128,128]{2,1,0:T(8,128)(2,1)S(1)}, u32[]{:S(2)}, u32[]{:S(2)}) %collective-permute-start.6) | collective-permute-done | bytes 262176 | tf_op jit(solution)/shard_map/ppermute | solution.py:13
  84.3 2.1 %multiply_reduce_fusion = f32[8,128,512]{2,1,0:T(8,128)S(1)} fusion(bf16[512,8,128,1]{0,2,3,1:T(8,128)(2,1)S(1)} %copy-done.8, f32[7,512]{1,0:T(8,128)S(1)} %get-tuple-element.23, bf16[7,8,128,128]{3,2,1,0:T(8,128)(2,1)S(1)} %fusion.49), kind=kOutput, calls=%fused_computation.5 | convolution fusion | flops 946339840 | bytes 4995072 | tf_op jit(solution)/shard_map/thd,lhde->lthe/dot_general | solution.py:96
  87.8 1.6 fusion.9
  89.4 1.7 copy.47
  91.1 5.5 %fusion.74 = (bf16[7,8,128,128]{3,2,0,1:T(8,128)(2,1)S(1)}, f32[7,8,128,128]{3,2,0,1:T(8,128)}) fusion(bf16[512,8,128,1]{0,2,3,1:T(8,128)(2,1)} %copy.63, f32[512,8,128]{2,0,1:T(8,128)} %copy.47, f32[7,512]{1,0:T(8,128)S(1)} %get-tuple-element.22), kind=kOutput, calls=%fused_computation.122 | convolution fusion | flops 947781632 | bytes 8665088 | tf_op jit(solution)/shard_map/thd,lthe->lhde/dot_general | solution.py:119
  96.7 1.5 copy.110
  98.2 4.8 %all-to-all-start = ((bf16[8,4,8,16,128]{4,3,1,2,0:T(8,128)(2,1)}), bf16[8,4,8,16,128]{4,3,1,2,0:T(8,128)(2,1)}, u32[]{:S(2)}, u32[]{:S(2)}) async-start(bf16[8,4,8,16,128]{4,3,1,2,0:T(8,128)(2,1)} %bitcast.153), calls=%async_computation | async-start | bytes 2097152 | tf_op jit(solution)/shard_map/all_to_all | solution.py:24
  103.3 2.1 %slice.92 = bf16[3,8,128,128]{3,2,0,1:T(8,128)(2,1)} slice(bf16[7,8,128,128]{3,2,0,1:T(8,128)(2,1)} %copy-done.5), slice={[0:3], [0:8], [0:128], [0:128]} | slice | bytes 1572864 | tf_op jit(solution)/shard_map/slice | solution.py:120
  105.4 2.0 %collective-permute-start.7 = (bf16[3,8,128,128]{3,2,0,1:T(8,128)(2,1)}, bf16[3,8,128,128]{3,2,0,1:T(8,128)(2,1)}, u32[]{:S(2)}, u32[]{:S(2)}) collective-permute-start(bf16[3,8,128,128]{3,2,0,1:T(8,128)(2,1)} %slice.92), channel_id=1, source_target_pairs={{0,1},{1,0},{2,3},{3,2},{4,5},{5,4},{6,7},{7,6},{8,9},{9,8},{10,11... | collective-permute-start | bytes 2359304 | tf_op jit(solution)/shard_map/ppermute | solution.py:13
  107.4 3.6 %select_convert_fusion = bf16[8,512,512]{2,1,0:T(8,128)(2,1)} fusion(pred[512,512]{1,0:T(8,128)(4,1)S(1)} %copy-done.14, bf16[512,8,128]{0,2,1:T(8,128)(2,1)S(1)} %get-tuple-element.15, f32[512]{0:T(512)S(1)} %bitcast.160, bf16[512,1024]{1,0:T(8,128)(2,1)S(1)} %copy-done), kind=kOutput, calls=%fused_computation.6 | convolution fusion | flops 544735232 | bytes 6555648 | tf_op jit(solution)/shard_map/the,she->hts/dot_general | solution.py:108
  111.0 4.0 %fusion.1 = (f32[7,512]{1,0:T(8,128)S(1)}, f32[512,8,128]{0,2,1:T(8,128)}) fusion(f32[512,8,128]{0,2,1:T(8,128)S(1)} %convert_element_type.213, f32[7,512]{1,0:T(8,128)S(1)} %get-tuple-element.23, bf16[512,8,128]{0,2,1:T(8,128)(2,1)S(1)} %get-tuple-element.15, bf16[7,8,128,128]{3,2,1,0:T(8,128)(2,1)S(1)} %copy-done.16), kind=kOutput, calls=%fused_computation.3 | convolution fusion | flops 953676288 | bytes 7106560 | tf_op jit(solution)/shard_map/the,lhde->lthd/dot_general | solution.py:100
  115.0 15.4 %all-to-all-done = bf16[8,4,8,16,128]{4,3,1,2,0:T(8,128)(2,1)} async-done(((bf16[8,4,8,16,128]{4,3,1,2,0:T(8,128)(2,1)}), bf16[8,4,8,16,128]{4,3,1,2,0:T(8,128)(2,1)}, u32[]{:S(2)}, u32[]{:S(2)}) %all-to-all-start) | async-done | bytes 1048608 | tf_op jit(solution)/shard_map/all_to_all | solution.py:24
  130.4 1.5 convert_reduce_fusion
  132.8 5.5 %fusion.6 = bf16[512,8,128]{0,2,1:T(8,128)(2,1)} fusion(f32[512,8,128]{0,2,1:T(8,128)} %get-tuple-element.13, bf16[8,512,512]{2,1,0:T(8,128)(2,1)} %select_convert_fusion, bf16[512,8,128]{0,2,1:T(8,128)(2,1)S(1)} %copy-done.10), kind=kOutput, calls=%fused_computation.14 | convolution fusion | flops 537919488 | bytes 8388608 | tf_op jit(solution)/shard_map/hts,shd->thd/dot_general | solution.py:112
  139.6 2.1 %fusion.25 = f32[8,128,512]{2,1,0:T(8,128)} fusion(bf16[8,512,512]{2,1,0:T(8,128)(2,1)S(1)} %copy-done.2, bf16[512,8,128]{0,2,1:T(8,128)(2,1)S(1)} %get-tuple-element.15, f32[512]{0:T(512)S(1)} %bitcast.161), kind=kOutput, calls=%fused_computation.43 | convolution fusion | flops 538443776 | bytes 7342080 | tf_op jit(solution)/shard_map/hts,the->she/dot_general | solution.py:142
  141.6 1.3 convert_element_type.191
  142.9 1.8 collective-permute-done.11
  145.9 2.4 %fusion.73 = (bf16[2,8,128,128]{3,2,0,1:T(8,128)(2,1)S(1)}, f32[2,8,128,128]{3,2,0,1:T(8,128)}) fusion(f32[3,8,128,128]{3,2,0,1:T(8,128)S(1)} %convert_element_type.191, f32[7,8,128,128]{3,2,0,1:T(8,128)} %get-tuple-element.25), kind=kLoop, calls=%fused_computation.121 | loop fusion | flops 524288 | bytes 3670016 | tf_op jit(solution)/shard_map/convert_element_type | solution.py:123
  149.2 2.0 %collective-permute-start.13 = (bf16[1,8,16,128]{3,2,0,1:T(8,128)(2,1)S(1)}, bf16[1,8,16,128]{3,2,0,1:T(8,128)(2,1)S(1)}, u32[]{:S(2)}, u32[]{:S(2)}) collective-permute-start(bf16[1,8,16,128]{3,2,0,1:T(8,128)(2,1)S(1)} %fusion.62), channel_id=1, source_target_pairs={{0,64},{8,72},{16,80},{24,88},{32,96},{40,104},{48,112},{56,120},{... | collective-permute-start | bytes 98312 | tf_op jit(solution)/shard_map/ppermute | solution.py:13
  151.3 3.4 %collective-permute-done.13 = bf16[1,8,16,128]{3,2,0,1:T(8,128)(2,1)S(1)} collective-permute-done((bf16[1,8,16,128]{3,2,0,1:T(8,128)(2,1)S(1)}, bf16[1,8,16,128]{3,2,0,1:T(8,128)(2,1)S(1)}, u32[]{:S(2)}, u32[]{:S(2)}) %collective-permute-start.13) | collective-permute-done | bytes 32800 | tf_op jit(solution)/shard_map/ppermute | solution.py:13
  155.5 4.3 %all-to-all-start.1 = ((bf16[8,8,16,128]{3,2,1,0:T(8,128)(2,1)}), bf16[8,8,16,128]{3,2,1,0:T(8,128)(2,1)S(1)}, u32[]{:S(2)}, u32[]{:S(2)}) async-start(bf16[8,8,16,128]{3,2,1,0:T(8,128)(2,1)} %broadcast_in_dim.67), calls=%async_computation.1 | async-start | bytes 524288 | tf_op jit(solution)/shard_map/all_to_all | solution.py:36
  159.8 12.4 %collective-permute-done.8 = bf16[2,8,128,128]{3,2,0,1:T(8,128)(2,1)} collective-permute-done((bf16[2,8,128,128]{3,2,0,1:T(8,128)(2,1)S(1)}, bf16[2,8,128,128]{3,2,0,1:T(8,128)(2,1)}, u32[]{:S(2)}, u32[]{:S(2)}) %collective-permute-start.8) | collective-permute-done | bytes 524320 | tf_op jit(solution)/shard_map/ppermute | solution.py:13
  173.4 1.8 fusion.38
  175.2 5.4 %collective-permute-start.9 = (bf16[1,8,128,128]{3,2,0,1:T(8,128)(2,1)}, bf16[1,8,128,128]{3,2,0,1:T(8,128)(2,1)}, u32[]{:S(2)}, u32[]{:S(2)}) collective-permute-start(bf16[1,8,128,128]{3,2,0,1:T(8,128)(2,1)} %fusion.38), channel_id=1, source_target_pairs={{0,4},{1,5},{2,6},{3,7},{4,0},{5,1},{6,2},{7,3},{8,12},{9,13},{10,... | collective-permute-start | bytes 786440 | tf_op jit(solution)/shard_map/ppermute | solution.py:13
  180.6 2.3 %copy.56 = bf16[512,1024]{1,0:T(8,128)(2,1)} copy(bf16[512,1024]{0,1:T(8,128)(2,1)} %bitcast.156) | data formatting | bytes 2097152
  182.9 3.9 %psum.7 = f32[8,512]{1,0:T(8,128)} all-reduce(f32[8,512]{1,0:T(8,128)S(1)} %pad_maximum_fusion), channel_id=1, replica_groups=mesh['head'=2,'outer'=16,'inner'=8] {'head'}, use_global_device_ids=true, to_apply=%region_5.6 | all-reduce | flops 4096 | bytes 32768 | tf_op jit(solution)/shard_map/psum | solution.py:106
  186.9 3.8 %collective-permute-done.9 = bf16[1,8,128,128]{3,2,0,1:T(8,128)(2,1)} collective-permute-done((bf16[1,8,128,128]{3,2,0,1:T(8,128)(2,1)}, bf16[1,8,128,128]{3,2,0,1:T(8,128)(2,1)}, u32[]{:S(2)}, u32[]{:S(2)}) %collective-permute-start.9) | collective-permute-done | bytes 262176 | tf_op jit(solution)/shard_map/ppermute | solution.py:13
  190.7 1.3 fusion.43
  192.0 1.7 fusion.16
  195.1 1.3 copy.58
  196.4 3.6 %fusion.5 = bf16[512,8,128]{0,2,1:T(8,128)(2,1)S(1)} fusion(f32[8,128,512]{2,1,0:T(8,128)} %fusion.16, bf16[512,8,128]{0,2,1:T(8,128)(2,1)S(1)} %copy.46, bf16[8,512,512]{2,1,0:T(8,128)(2,1)} %select_convert_fusion), kind=kOutput, calls=%fused_computation.12 | convolution fusion | flops 537919488 | bytes 8388608 | tf_op jit(solution)/shard_map/hts,thd->shd/dot_general | solution.py:139
  200.0 1.3 copy.57
  (89 shorter events, 21.2 us)
Async XLA Ops:
  0.6 2.3 %copy-start = (bf16[512,1024]{1,0:T(8,128)(2,1)S(1)}, bf16[512,1024]{1,0:T(8,128)(2,1)}, u32[]{:S(2)}) copy-start(bf16[512,1024]{1,0:T(8,128)(2,1)} %param.8) | copy-start | bytes 3145732
  2.9 12.8 %copy-start.9 = (bf16[512,8,128]{0,2,1:T(8,128)(2,1)}, bf16[512,8,128]{0,2,1:T(8,128)(2,1)S(1)}, u32[]{:S(2)}) copy-start(bf16[512,8,128]{0,2,1:T(8,128)(2,1)S(1)} %copy.36) | copy-start | bytes 3145732
  2.9 12.8 %copy-start.12 = (bf16[512,1024]{1,0:T(8,128)(2,1)S(1)}, bf16[512,1024]{1,0:T(8,128)(2,1)}, u32[]{:S(2)}) copy-start(bf16[512,1024]{1,0:T(8,128)(2,1)} %param.6) | copy-start | bytes 3145732
  3.4 12.7 %copy-start.11 = (bf16[8,128,128]{2,1,0:T(8,128)(2,1)}, bf16[8,128,128]{2,1,0:T(8,128)(2,1)S(1)}, u32[]{:S(2)}) copy-start(bf16[8,128,128]{2,1,0:T(8,128)(2,1)S(1)} %convolution_convert_fusion) | copy-start | bytes 786436
  3.4 8.3 %collective-permute-start = (bf16[8,128,128]{2,1,0:T(8,128)(2,1)S(1)}, bf16[8,128,128]{2,1,0:T(8,128)(2,1)S(1)}, u32[]{:S(2)}, u32[]{:S(2)}) collective-permute-start(bf16[8,128,128]{2,1,0:T(8,128)(2,1)S(1)} %convolution_convert_fusion), channel_id=1, source_target_pairs={{0,1},{1,0},{2,3},{3,2},{4,5},{5,4},{6,7},{7,6},{8,9},{9,8},{10,11... | collective-permute-start | bytes 786440 | tf_op jit(solution)/shard_map/ppermute | solution.py:13
  12.5 14.8 %collective-permute-start.1 = (bf16[8,128,128]{2,1,0:T(8,128)(2,1)}, bf16[8,128,128]{2,1,0:T(8,128)(2,1)}, u32[]{:S(2)}, u32[]{:S(2)}) collective-permute-start(bf16[8,128,128]{2,1,0:T(8,128)(2,1)} %fusion.44), channel_id=1, source_target_pairs={{0,2},{1,3},{2,0},{3,1},{4,6},{5,7},{6,4},{7,5},{8,10},{9,11},{10,... | collective-permute-start | bytes 786440 | tf_op jit(solution)/shard_map/ppermute | solution.py:13
  16.8 23.2 %copy-start.13 = (pred[512,512]{1,0:T(8,128)(4,1)}, pred[512,512]{1,0:T(8,128)(4,1)S(1)}, u32[]{:S(2)}) copy-start(pred[512,512]{1,0:T(8,128)(4,1)S(1)} %iota_compare_fusion) | copy-start | bytes 786436
  29.2 10.9 %copy-start.17 = (bf16[8,512]{1,0:T(8,128)(2,1)S(1)}, bf16[8,512]{1,0:T(8,128)(2,1)}, u32[]{:S(2)}) copy-start(bf16[8,512]{1,0:T(8,128)(2,1)} %param.10) | copy-start | bytes 24580
  29.2 10.9 %copy-start.19 = (f32[8]{0:T(128)S(1)}, f32[8]{0:T(128)}, u32[]{:S(2)}) copy-start(f32[8]{0:T(128)} %constant.80.clone) | copy-start | bytes 100
  29.2 18.2 %collective-permute-start.2 = (bf16[8,128,128]{2,1,0:T(8,128)(2,1)}, bf16[8,128,128]{2,1,0:T(8,128)(2,1)}, u32[]{:S(2)}, u32[]{:S(2)}) collective-permute-start(bf16[8,128,128]{2,1,0:T(8,128)(2,1)} %fusion.46), channel_id=1, source_target_pairs={{0,4},{1,5},{2,6},{3,7},{4,0},{5,1},{6,2},{7,3},{8,12},{9,13},{10,... | collective-permute-start | bytes 786440 | tf_op jit(solution)/shard_map/ppermute | solution.py:13
  49.3 8.6 %collective-permute-start.3 = (bf16[8,128,128]{2,1,0:T(8,128)(2,1)}, bf16[8,128,128]{2,1,0:T(8,128)(2,1)}, u32[]{:S(2)}, u32[]{:S(2)}) collective-permute-start(bf16[8,128,128]{2,1,0:T(8,128)(2,1)} %fusion.33), channel_id=1, source_target_pairs={{0,8},{8,0},{16,24},{24,16},{32,40},{40,32},{48,56},{56,48},{64,72... | collective-permute-start | bytes 786440 | tf_op jit(solution)/shard_map/ppermute | solution.py:13
  59.0 8.0 %collective-permute-start.4 = (bf16[8,128,128]{2,1,0:T(8,128)(2,1)S(1)}, bf16[8,128,128]{2,1,0:T(8,128)(2,1)S(1)}, u32[]{:S(2)}, u32[]{:S(2)}) collective-permute-start(bf16[8,128,128]{2,1,0:T(8,128)(2,1)S(1)} %fusion.45), channel_id=1, source_target_pairs={{0,16},{8,24},{16,0},{24,8},{32,48},{40,56},{48,32},{56,40},{64,80... | collective-permute-start | bytes 786440 | tf_op jit(solution)/shard_map/ppermute | solution.py:13
  68.1 16.2 %copy-start.8 = (bf16[512,8,128,1]{0,2,3,1:T(8,128)(2,1)S(1)}, bf16[512,8,128,1]{0,2,3,1:T(8,128)(2,1)}, u32[]{:S(2)}) copy-start(bf16[512,8,128,1]{0,2,3,1:T(8,128)(2,1)} %copy.63) | copy-start | bytes 3145732
  68.1 6.6 %collective-permute-start.5 = (bf16[8,128,128]{2,1,0:T(8,128)(2,1)S(1)}, bf16[8,128,128]{2,1,0:T(8,128)(2,1)S(1)}, u32[]{:S(2)}, u32[]{:S(2)}) collective-permute-start(bf16[8,128,128]{2,1,0:T(8,128)(2,1)S(1)} %fusion.47), channel_id=1, source_target_pairs={{0,32},{8,40},{16,48},{24,56},{32,0},{40,8},{48,16},{56,24},{64,96... | collective-permute-start | bytes 786440 | tf_op jit(solution)/shard_map/ppermute | solution.py:13
  75.9 8.3 %collective-permute-start.6 = (bf16[8,128,128]{2,1,0:T(8,128)(2,1)S(1)}, bf16[8,128,128]{2,1,0:T(8,128)(2,1)S(1)}, u32[]{:S(2)}, u32[]{:S(2)}) collective-permute-start(bf16[8,128,128]{2,1,0:T(8,128)(2,1)S(1)} %fusion.37), channel_id=1, source_target_pairs={{0,64},{8,72},{16,80},{24,88},{32,96},{40,104},{48,112},{56,120},{... | collective-permute-start | bytes 786440 | tf_op jit(solution)/shard_map/ppermute | solution.py:13
  84.3 2.2 %copy-start.15 = (bf16[7,8,128,128]{3,2,1,0:T(8,128)(2,1)}, bf16[7,8,128,128]{3,2,1,0:T(8,128)(2,1)S(1)}, u32[]{:S(2)}) copy-start(bf16[7,8,128,128]{3,2,1,0:T(8,128)(2,1)S(1)} %fusion.49) | copy-start | bytes 5505028
  84.3 2.9 %copy-start.1 = (bf16[8,512,512]{2,1,0:T(8,128)(2,1)S(1)}, bf16[8,512,512]{2,1,0:T(8,128)(2,1)}, u32[]{:S(2)}) copy-start(bf16[8,512,512]{2,1,0:T(8,128)(2,1)} %select_convert_fusion.1) | copy-start | bytes 12582916
  84.3 3.5 %copy-start.3 = (f32[512,1024]{0,1:T(8,128)S(1)}, f32[512,1024]{0,1:T(8,128)}, u32[]{:S(2)}) copy-start(f32[512,1024]{0,1:T(8,128)} %copy.40) | copy-start | bytes 6291460
  96.6 1.6 copy-start.5
  98.2 32.3 %all-to-all-start = ((bf16[8,4,8,16,128]{4,3,1,2,0:T(8,128)(2,1)}), bf16[8,4,8,16,128]{4,3,1,2,0:T(8,128)(2,1)}, u32[]{:S(2)}, u32[]{:S(2)}) async-start(bf16[8,4,8,16,128]{4,3,1,2,0:T(8,128)(2,1)} %bitcast.153), calls=%async_computation | async-start | bytes 2097152 | tf_op jit(solution)/shard_map/all_to_all | solution.py:24
  103.0 4.4 %copy-start.14 = (pred[512,512]{1,0:T(8,128)(4,1)S(1)}, pred[512,512]{1,0:T(8,128)(4,1)}, u32[]{:S(2)}) copy-start(pred[512,512]{1,0:T(8,128)(4,1)} %copy-done.13) | copy-start | bytes 786436
  105.4 5.6 %copy-start.16 = (bf16[7,8,128,128]{3,2,1,0:T(8,128)(2,1)S(1)}, bf16[7,8,128,128]{3,2,1,0:T(8,128)(2,1)}, u32[]{:S(2)}) copy-start(bf16[7,8,128,128]{3,2,1,0:T(8,128)(2,1)} %copy-done.15) | copy-start | bytes 5505028
  105.4 36.3 %collective-permute-start.7 = (bf16[3,8,128,128]{3,2,0,1:T(8,128)(2,1)}, bf16[3,8,128,128]{3,2,0,1:T(8,128)(2,1)}, u32[]{:S(2)}, u32[]{:S(2)}) collective-permute-start(bf16[3,8,128,128]{3,2,0,1:T(8,128)(2,1)} %slice.92), channel_id=1, source_target_pairs={{0,1},{1,0},{2,3},{3,2},{4,5},{5,4},{6,7},{7,6},{8,9},{9,8},{10,11... | collective-permute-start | bytes 2359304 | tf_op jit(solution)/shard_map/ppermute | solution.py:13
  130.4 2.4 %copy-start.10 = (bf16[512,8,128]{0,2,1:T(8,128)(2,1)S(1)}, bf16[512,8,128]{0,2,1:T(8,128)(2,1)}, u32[]{:S(2)}) copy-start(bf16[512,8,128]{0,2,1:T(8,128)(2,1)} %copy-done.9) | copy-start | bytes 3145732
  132.0 6.3 %collective-permute-start.10 = (bf16[4,8,16,128]{3,2,0,1:T(8,128)(2,1)S(1)}, bf16[4,8,16,128]{3,2,0,1:T(8,128)(2,1)S(1)}, u32[]{:S(2)}, u32[]{:S(2)}) collective-permute-start(bf16[4,8,16,128]{3,2,0,1:T(8,128)(2,1)S(1)} %convert_element_type.197), channel_id=1, source_target_pairs={{0,8},{8,0},{16,24},{24,16},{32,40},{40,32},{48,56},{56,48},{64,72... | collective-permute-start | bytes 393224 | tf_op jit(solution)/shard_map/ppermute | solution.py:13
  132.8 6.8 %copy-start.2 = (bf16[8,512,512]{2,1,0:T(8,128)(2,1)S(1)}, bf16[8,512,512]{2,1,0:T(8,128)(2,1)}, u32[]{:S(2)}) copy-start(bf16[8,512,512]{2,1,0:T(8,128)(2,1)} %select_convert_fusion.1) | copy-start | bytes 12582916
  138.3 6.4 %collective-permute-start.11 = (bf16[3,8,16,128]{3,2,0,1:T(8,128)(2,1)S(1)}, bf16[3,8,16,128]{3,2,0,1:T(8,128)(2,1)S(1)}, u32[]{:S(2)}, u32[]{:S(2)}) collective-permute-start(bf16[3,8,16,128]{3,2,0,1:T(8,128)(2,1)S(1)} %get-tuple-element.18), channel_id=1, source_target_pairs={{0,16},{8,24},{16,0},{24,8},{32,48},{40,56},{48,32},{56,40},{64,80... | collective-permute-start | bytes 294920 | tf_op jit(solution)/shard_map/ppermute | solution.py:13
  142.9 5.4 %copy-start.6 = (f32[3,8,128,128]{3,2,0,1:T(8,128)}, f32[3,8,128,128]{3,2,0,1:T(8,128)S(1)}, u32[]{:S(2)}) copy-start(f32[3,8,128,128]{3,2,0,1:T(8,128)S(1)} %convert_element_type.191) | copy-start | bytes 4718596
  144.8 6.4 %copy-start.18 = (f32[7]{0:T(128)S(1)}, f32[7]{0:T(128)}, u32[]{:S(2)}) copy-start(f32[7]{0:T(128)} %constant.83) | copy-start | bytes 88
  144.8 4.4 %collective-permute-start.12 = (bf16[2,8,16,128]{3,2,0,1:T(8,128)(2,1)S(1)}, bf16[2,8,16,128]{3,2,0,1:T(8,128)(2,1)S(1)}, u32[]{:S(2)}, u32[]{:S(2)}) collective-permute-start(bf16[2,8,16,128]{3,2,0,1:T(8,128)(2,1)S(1)} %get-tuple-element.16), channel_id=1, source_target_pairs={{0,32},{8,40},{16,48},{24,56},{32,0},{40,8},{48,16},{56,24},{64,96... | collective-permute-start | bytes 196616 | tf_op jit(solution)/shard_map/ppermute | solution.py:13
  148.3 23.9 %collective-permute-start.8 = (bf16[2,8,128,128]{3,2,0,1:T(8,128)(2,1)S(1)}, bf16[2,8,128,128]{3,2,0,1:T(8,128)(2,1)}, u32[]{:S(2)}, u32[]{:S(2)}) collective-permute-start(bf16[2,8,128,128]{3,2,0,1:T(8,128)(2,1)S(1)} %get-tuple-element.20), channel_id=1, source_target_pairs={{0,2},{1,3},{2,0},{3,1},{4,6},{5,7},{6,4},{7,5},{8,10},{9,11},{10,... | collective-permute-start | bytes 1572872 | tf_op jit(solution)/shard_map/ppermute | solution.py:13
  149.2 5.5 %collective-permute-start.13 = (bf16[1,8,16,128]{3,2,0,1:T(8,128)(2,1)S(1)}, bf16[1,8,16,128]{3,2,0,1:T(8,128)(2,1)S(1)}, u32[]{:S(2)}, u32[]{:S(2)}) collective-permute-start(bf16[1,8,16,128]{3,2,0,1:T(8,128)(2,1)S(1)} %fusion.62), channel_id=1, source_target_pairs={{0,64},{8,72},{16,80},{24,88},{32,96},{40,104},{48,112},{56,120},{... | collective-permute-start | bytes 98312 | tf_op jit(solution)/shard_map/ppermute | solution.py:13
  155.5 31.4 %all-to-all-start.1 = ((bf16[8,8,16,128]{3,2,1,0:T(8,128)(2,1)}), bf16[8,8,16,128]{3,2,1,0:T(8,128)(2,1)S(1)}, u32[]{:S(2)}, u32[]{:S(2)}) async-start(bf16[8,8,16,128]{3,2,1,0:T(8,128)(2,1)} %broadcast_in_dim.67), calls=%async_computation.1 | async-start | bytes 524288 | tf_op jit(solution)/shard_map/all_to_all | solution.py:36
  175.2 15.5 %collective-permute-start.9 = (bf16[1,8,128,128]{3,2,0,1:T(8,128)(2,1)}, bf16[1,8,128,128]{3,2,0,1:T(8,128)(2,1)}, u32[]{:S(2)}, u32[]{:S(2)}) collective-permute-start(bf16[1,8,128,128]{3,2,0,1:T(8,128)(2,1)} %fusion.38), channel_id=1, source_target_pairs={{0,4},{1,5},{2,6},{3,7},{4,0},{5,1},{6,2},{7,3},{8,12},{9,13},{10,... | collective-permute-start | bytes 786440 | tf_op jit(solution)/shard_map/ppermute | solution.py:13
  191.9 1.9 copy-start.4
  191.9 2.6 %copy-start.7 = (bf16[512,1024]{1,0:T(8,128)(2,1)S(1)}, bf16[512,1024]{1,0:T(8,128)(2,1)}, u32[]{:S(2)}) copy-start(bf16[512,1024]{1,0:T(8,128)(2,1)} %param.7) | copy-start | bytes 3145732
where the time goes:
time: 203 us; the launch traced here: 201 us
  waiting for transfers between devices  79.6 us (39%)
  starting transfers between devices  39.1 us (19%)
  matrix products  35.4 us (17%)
  other arithmetic  21.6 us (11%)
  local copies, waits for them, and re-layouts  20.6 us (10%)
  blocking collectives  3.94 us (2%)
    ppermute x14, waiting for transfers between devices, partner_2(): return lax.ppermute(value, axis, pairs)  64.2 us
    ppermute x14, starting transfers between devices, partner_2(): return lax.ppermute(value, axis, pairs)  30 us
    all_to_all x1, waiting for transfers between devices, sent_and_summed(): lax.all_to_all(parts, axis, split_axis=0, concat_axis=0, tiled=True)  15.4 us
    unnamed x45, local copies, waits for them, and re-layouts  9.02 us
    convert_element_type x5, other arithmetic, on_device(): running.astype(jnp.bfloat16)  6.02 us
    dot_general x1, matrix products, on_device(): jnp.einsum('thd,lthe->lhde', query3, weighted, preferred_element_type=jnp...  5.52 us
    dot_general x1, matrix products, on_device(): jnp.einsum('hts,shd->thd', score_grad, key3, preferred_element_type=jnp.f...  5.46 us
    all_to_all x1, starting transfers between devices, sent_and_summed(): lax.all_to_all(parts, axis, split_axis=0, concat_axis=0, tiled=True)  4.82 us
  transfers between devices with their start and end apart: 16, of which 13 were waited for; matrix products, arithmetic and copies ran while one was open for 21% of the time, Pallas kernels for 0%

commit v1 on v0

v1 whole, which is shorter than its diff:
```python
import functools

import jax
import jax.numpy as jnp
from jax import lax
from jax.experimental import pallas as pl
from jax.experimental.pallas import tpu as pltpu
from jax.sharding import PartitionSpec as P

DK = 128
MESH = pl.DeviceIdType.MESH
F32 = jnp.float32
BF16 = jnp.bfloat16


def nn(a, b):
    return lax.dot_general(a, b, (((1,), (0,)), ((), ())), preferred_element_type=F32)


def nt(a, b):
    return lax.dot_general(a, b, (((1,), (1,)), ((), ())), preferred_element_type=F32)


def tn(a, b):
    return lax.dot_general(a, b, (((0,), (0,)), ((), ())), preferred_element_type=F32)


def bit_of(number, position):
    return lax.rem(lax.div(number, 2**position), 2)


def kernel(
    dims,
    q_hbm, k_hbm, v_hbm, y_hbm, w_hbm,
    gq_hbm, gk_hbm, gv_hbm, gl_hbm,
    Q, K, V, Y, W, BS, FR, LS, IS, TOT, YR, YT, XR, COEF, QC, SC, IN, ER, AD,
    AL1, AI, RP, BXS, BXR, BYS, BYR, DS, BA, GK, GV, OQ, OK, OV, GACC, GLP, GLR,
    in_sem, w_sem, out_sem, gl_sem,
    f1s, f1r, fl1, f2s, f2r, fys, fyr, fxs, fxr, f3s, f3r,
    bl1, b2s, b2r, b3s, b3r, bxs, bxr, bys, byr, b4s, b4r, glx,
):
    n, nlo, nhi, nhead, ib, lob, hib, rows, scales, gamma = dims
    ob = lob + hib
    nb = ib + ob
    half = n // 2
    p = lax.axis_index("inner")
    g = lax.axis_index("outer")
    hd = lax.axis_index("head")
    x = lax.div(g, nlo)
    y = lax.rem(g, nlo)

    def zdev(r):
        return (hd, g, r)

    def odev(o):
        return (hd, o, p)

    def ydev(yy):
        return odev(x * nlo + yy)

    def xdev(xx):
        return odev(xx * nlo + y)

    def wrap(i):
        return lax.rem(i + 2 * n, n)

    def loop(count, body, unroll=1):
        def step(i, c):
            body(i)
            return c
        lax.fori_loop(0, count, step, 0, unroll=unroll)

    def rc(src, dst, ss, rs, dev):
        return pltpu.make_async_remote_copy(
            src_ref=src, dst_ref=dst, send_sem=ss, recv_sem=rs, device_id=dev, device_id_type=MESH
        )

    def cols(h):
        return pl.ds(pl.multiple_of(h * DK, DK), DK)

    def lev(b):
        return pl.ds(b * DK, DK)

    def in_copy(a, h):
        hbm, vm = ((k_hbm, K), (v_hbm, V), (q_hbm, Q), (y_hbm, Y))[a]
        return pltpu.make_async_copy(hbm.at[:, cols(h)], vm.at[h], in_sem.at[a, h])

    def out_copy(a, h):
        hbm, vm = ((gq_hbm, OQ), (gk_hbm, OK), (gv_hbm, OV))[a]
        return pltpu.make_async_copy(vm.at[h], hbm.at[:, cols(h)], out_sem.at[a, h])

    def start_kv(h):
        in_copy(0, h).start()
        in_copy(1, h).start()

    def start_qy(h):
        in_copy(2, h).start()
        in_copy(3, h).start()

    loop(n, start_kv)
    w_copy = pltpu.make_async_copy(w_hbm, W, w_sem)
    w_copy.start()
    loop(n, start_qy)

    barrier = pltpu.get_barrier_semaphore()

    def greet(dev):
        pl.semaphore_signal(barrier, inc=1, device_id=dev, device_id_type=MESH)

    loop(n - 1, lambda i: greet(zdev(wrap(p + 1 + i))))
    loop(nlo - 1, lambda i: greet(ydev(lax.rem(y + 1 + i, nlo))))
    loop(nhi - 1, lambda i: greet(xdev(lax.rem(x + 1 + i, nhi))))
    if nhead == 2:
        greet((1 - hd, g, p))

    def state(i):
        h = wrap(p + half + i)
        in_copy(0, h).wait()
        in_copy(1, h).wait()
        BS[h] = tn(K[h], V[h]).astype(BF16)

    loop(n, state, unroll=2)
    pl.semaphore_wait(barrier, (n - 1) + (nlo - 1) + (nhi - 1) + (nhead - 1))

    def f1(h, src):
        return rc(BS.at[h], FR.at[src], f1s.at[h], f1r.at[src], zdev(h))

    def f1_start(i):
        f1(wrap(p + half + i), p).start()

    loop(half, f1_start)
    loop(half - 1, lambda i: f1(wrap(p + 1 + i), p).start())
    fl1_copy = rc(BS, LS.at[:, lev(0), :], fl1.at[0], fl1.at[1], zdev(wrap(p + 1)))
    low0 = bit_of(p, 0) == 0

    @pl.when(low0)
    def _():
        fl1_copy.start()

    FR[p] = BS[p]

    w_copy.wait()
    for b in range(nb):
        bit = bit_of(p, b) if b < ib else bit_of(g, b - ib)

        @pl.when(bit == 0)
        def _():
            LS[:, lev(b), :] = jnp.zeros((n, DK, DK), BF16)

    weights = W[...]
    pick = lax.broadcasted_iota(jnp.int32, (nb + 1, DK), 0)
    for num in range(nb + 1):
        COEF[num] = tn(weights, jnp.where(pick == num, 1.0, 0.0).astype(BF16)) * scales[num]
    GACC[...] = jnp.zeros_like(GACC)

    def lower():
        return lax.broadcasted_iota(jnp.int32, (rows, rows), 0) >= lax.broadcasted_iota(
            jnp.int32, (rows, rows), 1
        )

    def ahead(h):
        in_copy(2, h).wait()
        in_copy(3, h).wait()
        query = Q[h]
        scores = nt(query, K[h]) * gamma
        kept = jnp.where(lower(), scores, 0.0).astype(BF16)
        SC[h] = kept
        IN[h] = nn(kept, V[h])
        query32 = query.astype(F32)
        for b in range(nb):
            QC[h, :, lev(b)] = (query32 * COEF[b + 1]).astype(BF16)

    loop(n, ahead)

    def f1_wait(i):
        src = wrap(p + 1 + i)
        f1(src, src).wait_recv()

    loop(n - 1, f1_wait)
    states = [FR[i].astype(F32) for i in range(n)]
    total = sum(states[1:], states[0])
    TOT[...] = total.astype(BF16)
    for b in range(1, ib):
        for node in range(n // 2 ** (b + 1)):
            first = node * 2 ** (b + 1)
            members = states[first : first + 2**b]
            IS[b - 1, node] = sum(members[1:], members[0]).astype(BF16)
    YR[y] = TOT[...]

    def fy(j, src):
        return rc(TOT, YR.at[src], fys.at[j], fyr.at[src], ydev(lax.rem(y + 1 + j, nlo)))

    loop(nlo - 1, lambda j: fy(j, y).start())

    def f2(b, dst, src):
        node = lax.div(dst, 2 ** (b + 1))
        return rc(
            IS.at[b - 1, node], LS.at[src, lev(b), :], f2s.at[b - 1, dst], f2r.at[b - 1, src], zdev(dst)
        )

    for b in range(1, ib):
        def f2_start(i):
            dst = wrap(p + 1 + i)

            @pl.when(bit_of(dst, b) == 1)
            def _():
                f2(b, dst, p).start()

        loop(n - 1, f2_start)

        @pl.when(bit_of(p, b) == 1)
        def _():
            LS[p, lev(b), :] = IS[b - 1, lax.div(p, 2 ** (b + 1))]

    def masked_sum(ref, count, me, m):
        out = jnp.zeros((DK, DK), F32)
        for i in range(count):
            cond = (
                (bit_of(me, m) == 1)
                & (lax.div(me, 2 ** (m + 1)) == i >> (m + 1))
                & ((i >> m) % 2 == 0)
            )
            out = out + jnp.where(cond, ref[i].astype(F32), 0.0)
        return out

    def f3(way, m, s, head):
        dst = wrap(p + 1) if way == 0 else wrap(p - 1)
        slot = LS.at[head, lev(ib + m), :]
        return rc(slot, slot, f3s.at[way, m, s], f3r.at[way, m, s], zdev(dst))

    hops = (half, half - 1)

    def on_bit(m, body):
        @pl.when(bit_of(g, m) == 1)
        def _():
            body()

    def f3_step(m, s):
        for way in range(2):
            if s > 0 and s - 1 < hops[way]:
                head = wrap(p - s) if way == 0 else wrap(p + s)
                f3(way, m, s - 1, head).wait_recv()
            if s < hops[way]:
                head = wrap(p - s) if way == 0 else wrap(p + s)
                f3(way, m, s, head).start()

    def fy_wait(j):
        src = lax.rem(y + 1 + j, nlo)
        fy(j, src).wait_recv()

    loop(nlo - 1, fy_wait)
    for m in range(lob):
        on_bit(m, lambda: LS.__setitem__((p, lev(ib + m)), masked_sum(YR, nlo, y, m).astype(BF16)))
    parts = [YR[i].astype(F32) for i in range(nlo)]
    YT[...] = sum(parts[1:], parts[0]).astype(BF16)
    for m in range(lob):
        on_bit(m, lambda: f3_step(m, 0))

    def fx(dst, src):
        return rc(YT, XR.at[src], fxs.at[dst], fxr.at[src], xdev(dst))

    def fx_start(j):
        @pl.when(x + 1 + j < nhi)
        def _():
            fx(x + 1 + j, x).start()

    def fx_wait(j):
        @pl.when(j < x)
        def _():
            fx(j, j).wait_recv()

    loop(nhi - 1, fx_start)
    loop(nhi - 1, fx_wait)
    for m in range(hib):
        on_bit(lob + m, lambda: LS.__setitem__((p, lev(ib + lob + m)), masked_sum(XR, nhi, x, m).astype(BF16)))
    for m in range(hib):
        on_bit(lob + m, lambda: f3_step(lob + m, 0))

    @pl.when(bit_of(p, 0) == 1)
    def _():
        fl1_copy.wait_recv()

    def b2(b, dst, src):
        return rc(AD.at[dst, b], AI.at[b - 1, src], b2s.at[b - 1, dst], b2r.at[b - 1, src], zdev(dst))

    def finish(h):
        inter = nn(QC[h], LS[h])
        error = (COEF[0] * IN[h] + inter - Y[h].astype(F32)).astype(BF16)
        ER[h] = error
        adjoint = tn(error, QC[h]).astype(BF16)
        for b in range(nb):
            AD[h, b] = adjoint[:, b * DK : (b + 1) * DK]

    def far(h):
        for b in range(1, ib):
            @pl.when(bit_of(p, b) == 1)
            def _():
                f2(b, p, h).wait_recv()
        finish(h)

    def far_send(h):
        for b in range(1, ib):
            @pl.when(bit_of(p, b) == 1)
            def _():
                b2(b, h, p).start()

    finish(p)
    for b in range(1, ib):
        @pl.when(bit_of(p, b) == 1)
        def _():
            AI[b - 1, p] = AD[p, b]

    for s in range(1, half + 1):
        for m in range(ob):
            on_bit(m, lambda: f3_step(m, s))
        heads = [wrap(p - s)] + ([wrap(p + s)] if s < half else [])
        def both(i):
            h = wrap(p - s + 2 * s * i)
            far(h)
        loop(len(heads), both)
        for h in heads:
            far_send(h)

    def b3(way, m, s):
        head = wrap(p + half - s) if way == 0 else wrap(p - (half - 1) + s)
        dst = wrap(p + 1) if way == 0 else wrap(p - 1)
        return rc(
            AD.at[head, ib + m], RP.at[way, m, s], b3s.at[way, m, s], b3r.at[way, m, s], zdev(dst)
        )

    def b3_step(m, s):
        for way in range(2):
            if s < hops[way]:
                if s > 0:
                    b3(way, m, s - 1).wait_recv()
                    head = wrap(p + half - s) if way == 0 else wrap(p - (half - 1) + s)
                    AD[head, ib + m] = (
                        AD[head, ib + m].astype(F32) + RP[way, m, s - 1].astype(F32)
                    ).astype(BF16)
                b3(way, m, s).start()

    for m in range(ob):
        on_bit(m, lambda: b3_step(m, 0))

    bl1_copy = rc(AD.at[:, 0], AL1, bl1.at[0], bl1.at[1], zdev(wrap(p - 1)))

    @pl.when(bit_of(p, 0) == 1)
    def _():
        bl1_copy.start()

    def heavy(h):
        error = ER[h]
        error32 = error.astype(F32)
        query = Q[h]
        query32 = query.astype(F32)
        key = K[h]
        intra_error = (COEF[0] * error32).astype(BF16)
        raw = nt(intra_error, V[h]) * gamma
        score_grad = jnp.where(lower(), raw, 0.0).astype(BF16)
        back = nt(error, LS[h])
        grad = nn(score_grad, key)
        GACC[0] += error32 * IN[h]
        for b in range(nb):
            piece = back[:, b * DK : (b + 1) * DK]
            grad = grad + COEF[b + 1] * piece
            GACC[b + 1] += query32 * piece
        OQ[h] = grad.astype(BF16)
        GK[h] = tn(score_grad, query)
        GV[h] = tn(SC[h], intra_error)

    per_step = n // (half + 1) if half > 1 else 1
    done = 0

    def some(count):
        nonlocal done
        count = min(count, n - done)
        first = done
        if count > 0:
            loop(count, lambda i: heavy(first + i))
        done = first + count

    for s in range(1, half):
        some(per_step)
        for m in range(ob):
            on_bit(m, lambda: b3_step(m, s))
    some(per_step)

    def own(m):
        value = AD[p, ib + m].astype(F32) + RP[0, m, hops[0] - 1].astype(F32)
        if hops[1] > 0:
            value = value + RP[1, m, hops[1] - 1].astype(F32)
        return value

    for m in reversed(range(ob)):
        def own_wait():
            for way in range(2):
                if hops[way] > 0:
                    b3(way, m, hops[way] - 1).wait_recv()
            if m >= lob:
                BXS[m - lob] = own(m).astype(BF16)
        on_bit(m, own_wait)

    def bx(m, dst, src):
        return rc(BXS.at[m], BXR.at[src], bxs.at[dst], bxr.at[src], xdev(dst))

    def top_bit(a, b, m):
        return (lax.div(a, 2 ** (m + 1)) == lax.div(b, 2 ** (m + 1))) & (
            lax.div(a, 2**m) != lax.div(b, 2**m)
        )

    for j in range(nhi - 1):
        for m in range(hib):
            @pl.when((j < x) & top_bit(x, jnp.int32(j), m))
            def _():
                bx(m, j, x).start()

    some(1)

    for j in range(1, nhi):
        @pl.when(j > x)
        def _():
            bx(0, 0, j).wait_recv()

    outer = jnp.zeros((DK, DK), F32)
    for j in range(1, nhi):
        outer = outer + jnp.where(j > x, BXR[j].astype(F32), 0.0)
    BYS[0] = outer.astype(BF16)
    for m in range(lob):
        @pl.when(bit_of(y, m) == 1)
        def _():
            BYS[m + 1] = (outer + own(m)).astype(BF16)

    def by(kind, dst, src):
        return rc(BYS.at[kind], BYR.at[src], bys.at[dst], byr.at[src], ydev(dst))

    for j in range(nlo):
        @pl.when(j > y)
        def _():
            by(0, j, y).start()
        for m in range(lob):
            @pl.when((j < y) & top_bit(y, jnp.int32(j), m))
            def _():
                by(m + 1, j, y).start()

    some(1)

    for b in range(1, ib):
        def b2_wait(i):
            src = wrap(p + 1 + i)

            @pl.when(bit_of(src, b) == 1)
            def _():
                b2(b, src, src).wait_recv()

        loop(n - 1, b2_wait)

    for j in range(nlo):
        @pl.when(j != y)
        def _():
            by(0, j, j).wait_recv()
    for j in range(nlo):
        outer = outer + jnp.where(j != y, BYR[j].astype(F32), 0.0)
    nodes = {}
    for b in range(1, ib):
        for node in range(n // 2 ** (b + 1)):
            first = node * 2 ** (b + 1) + 2**b
            members = [AI[b - 1, c].astype(F32) for c in range(first, first + 2**b)]
            nodes[b, node] = sum(members[1:], members[0])
    for dst in range(n):
        value = outer
        for b in range(1, ib):
            if (dst >> b) % 2 == 0:
                value = value + nodes[b, dst >> (b + 1)]
        DS[dst] = value.astype(BF16)
    BA[p] = DS[p]

    def b4(dst, src):
        return rc(DS.at[dst], BA.at[src], b4s.at[dst], b4r.at[src], zdev(dst))

    loop(half, lambda i: b4(wrap(p + half + i), p).start())
    loop(half - 1, lambda i: b4(wrap(p + 1 + i), p).start())
    some(n)

    row = lax.broadcasted_iota(jnp.int32, (nb + 1, rows), 0)
    ones = jnp.ones((nb + 1, DK), F32)
    mine = jnp.zeros((nb + 1, rows), F32)
    for num in range(nb + 1):
        sums = lax.dot_general(
            ones, GACC[num], (((1,), (1,)), ((), ())),
            precision=lax.Precision.HIGHEST, preferred_element_type=F32,
        )
        mine = jnp.where(row == num, sums * scales[num], mine)
    GLP[...] = mine
    loop(n, lambda h: out_copy(0, h).start())
    if nhead == 2:
        glx_copy = rc(GLP, GLR, glx.at[0], glx.at[1], (1 - hd, g, p))
        glx_copy.start()

    @pl.when(low0)
    def _():
        bl1_copy.wait_recv()

    def last(i):
        h = wrap(p + i)

        @pl.when(i > 0)
        def _():
            b4(h, h).wait_recv()
        adjoint = BA[h].astype(F32) + jnp.where(low0, AL1[h].astype(F32), 0.0)
        low = adjoint.astype(BF16)
        OK[h] = (GK[h] + nn(V[h], low)).astype(BF16)
        OV[h] = (GV[h] + nt(K[h], low)).astype(BF16)
        out_copy(1, h).start()
        out_copy(2, h).start()

    loop(n, last)

    if nhead == 2:
        glx_copy.wait_recv()
        glx_copy.wait_send()
        GLP[...] = GLP[...] + GLR[...]
    gl_copy = pltpu.make_async_copy(GLP, gl_hbm, gl_sem)
    gl_copy.start()

    loop(n - 1, lambda i: f1(wrap(p + 1 + i), p).wait_send())

    @pl.when(low0)
    def _():
        fl1_copy.wait_send()

    @pl.when(bit_of(p, 0) == 1)
    def _():
        bl1_copy.wait_send()

    loop(nlo - 1, lambda j: fy(j, y).wait_send())

    def fx_sent(j):
        @pl.when(x + 1 + j < nhi)
        def _():
            fx(x + 1 + j, x).wait_send()

    loop(nhi - 1, fx_sent)
    for b in range(1, ib):
        def sent(i):
            dst = wrap(p + 1 + i)

            @pl.when(bit_of(dst, b) == 1)
            def _():
                f2(b, dst, p).wait_send()

            @pl.when(bit_of(p, b) == 1)
            def _():
                b2(b, dst, p).wait_send()

        loop(n - 1, sent)
    for m in range(ob):
        def chain_sent():
            for way in range(2):
                for s in range(hops[way]):
                    f3(way, m, s, wrap(p - s) if way == 0 else wrap(p + s)).wait_send()
                    b3(way, m, s).wait_send()
        on_bit(m, chain_sent)
    for j in range(nhi - 1):
        @pl.when(j < x)
        def _():
            bx(0, j, x).wait_send()
    for j in range(nlo):
        @pl.when(j != y)
        def _():
            by(0, j, y).wait_send()
    loop(n - 1, lambda i: b4(wrap(p + 1 + i), p).wait_send())

    def written(h):
        for a in range(3):
            out_copy(a, h).wait()

    loop(n, written)
    gl_copy.wait()


def on_device(queries, key_rows, value_rows, teacher_out, level_weights):
    rows, width = queries.shape
    heads = width // DK
    n = lax.axis_size("inner")
    outer_count = lax.axis_size("outer")
    nhead = lax.axis_size("head")
    assert heads == n
    ib = n.bit_length() - 1
    ob = outer_count.bit_length() - 1
    lob = ob // 2
    hib = ob - lob
    nlo, nhi = 2**lob, 2**hib
    nb = ib + ob
    levels = level_weights.shape[0]
    assert levels == nb + 1
    gamma = DK ** (-0.5)
    scales = [rows ** (-0.5)] + [gamma * (rows * 2 ** (num - 1)) ** (-0.5) for num in range(1, levels)]
    dims = (n, nlo, nhi, nhead, ib, lob, hib, rows, tuple(scales), gamma)
    half = n // 2
    ibx = max(ib - 1, 1)
    any_spec = pl.BlockSpec(memory_space=pl.ANY)
    dma = pltpu.SemaphoreType.DMA

    def low(*shape):
        return pltpu.VMEM(shape, BF16)

    def wide(*shape):
        return pltpu.VMEM(shape, F32)

    sq = (DK, DK)
    scratch = [
        low(n, rows, DK), low(n, rows, DK), low(n, rows, DK), low(n, rows, DK), low(levels, rows),
        low(n, *sq), low(n, *sq), low(n, nb * DK, DK), low(ibx, max(n // 4, 1), *sq),
        low(*sq), low(nlo, *sq), low(*sq), low(nhi, *sq),
        wide(levels, rows, DK), low(n, rows, nb * DK), low(n, rows, rows), wide(n, rows, DK),
        low(n, rows, DK), low(n, nb, *sq),
        low(n, *sq), low(ibx, n, *sq), low(2, ob, half, *sq), low(hib, *sq), low(nhi, *sq),
        low(lob + 1, *sq), low(nlo, *sq), low(n, *sq), low(n, *sq),
        wide(n, rows, DK), wide(n, rows, DK), low(n, rows, DK), low(n, rows, DK), low(n, rows, DK),
        wide(levels, rows, DK), wide(levels, rows), wide(levels, rows),
        dma((4, n)), dma(()), dma((3, n)), dma(()),
        dma((n,)), dma((n,)), dma((2,)), dma((ibx, n)), dma((ibx, n)),
        dma((nlo,)), dma((nlo,)), dma((nhi,)), dma((nhi,)), dma((2, ob, half)), dma((2, ob, half)),
        dma((2,)), dma((ibx, n)), dma((ibx, n)), dma((2, ob, half)), dma((2, ob, half)),
        dma((nhi,)), dma((nhi,)), dma((nlo,)), dma((nlo,)), dma((n,)), dma((n,)), dma((2,)),
    ]
    big = jax.ShapeDtypeStruct((rows, width), BF16)
    return pl.pallas_call(
        functools.partial(kernel, dims),
        out_shape=(big, big, big, jax.ShapeDtypeStruct((levels, rows), F32)),
        in_specs=[any_spec] * 5,
        out_specs=[any_spec] * 4,
        scratch_shapes=scratch,
        compiler_params=pltpu.CompilerParams(
            collective_id=0, has_side_effects=True, vmem_limit_bytes=60 * 2**20
        ),
        name="log_linear",
    )(queries, key_rows, value_rows, teacher_out, level_weights)


def solution(mesh):
    tokens = P(("outer", "inner"), "head")
    per_token = P(None, ("outer", "inner"))
    return jax.shard_map(
        on_device,
        mesh=mesh,
        in_specs=(tokens, tokens, tokens, tokens, per_token),
        out_specs=(tokens, tokens, tokens, per_token),
        check_vma=False,
    )
```

time: 203 us -> 90.8 us (0.45)
  the two profiles are of different devices: /device:TPU:30 before, /device:TPU:32 now
where the time goes in v1:
time: 90.8 us; the launch traced here: 90.6 us
  Pallas kernels  84.4 us (93%)
  local copies, waits for them, and re-layouts  5.54 us (6%)
    pallas_call x1, Pallas kernels, on_device(): pl.pallas_call(functools.partial(kernel, dims), out_shape=(big, big, big,...  84.4 us
    unnamed x10, local copies, waits for them, and re-layouts  5.54 us

profile of v1, /device:TPU:32, one launch (start us, length us, event | category | flops | bytes accessed | tf_op | source)
XLA Modules:
  0.0 90.6 jit_solution(12561134409673098000)
XLA Ops:
  0.6 84.4 %log_linear.1 = (bf16[512,1024]{1,0:T(8,128)(2,1)}, bf16[512,1024]{1,0:T(8,128)(2,1)}, bf16[512,1024]{1,0:T(8,128)(2,1)}, f32[8,512]{1,0:T(8,128)}) custom-call(bf16[512,1024]{1,0:T(8,128)(2,1)} %q_hbm.1, bf16[512,1024]{1,0:T(8,128)(2,1)} %k_hbm.1, bf16[512,1024]{1,0:T(8,128)(2,1)} %v_hbm.1, bf16[512,1024]{1,0:T(8,128)(2,1)} %y_hbm.1, bf16[8,512]{1,0:T(8,128)(2,1)} %w_hbm.1), custom_call_target="tpu_custom_call" | custom-call | tf_op jit(solution)/shard_map/log_linear/pallas_call | solution.py:628
  85.1 0.0 copy-start.1
  85.1 2.4 %copy.13 = bf16[512,1024]{1,0:T(8,128)(2,1)} copy(bf16[512,1024]{1,0:T(8,128)(2,1)} %get-tuple-element.8) | data formatting | bytes 2097152
  87.4 0.0 copy-done.1
  87.4 0.0 copy-start
  87.4 1.0 %copy.14 = bf16[512,1024]{1,0:T(8,128)(2,1)} copy(bf16[512,1024]{1,0:T(8,128)(2,1)S(1)} %copy-done.1) | data formatting | bytes 2097152
  88.4 0.6 copy-done
  89.0 0.0 copy-start.2
  89.0 1.0 %copy.15 = bf16[512,1024]{1,0:T(8,128)(2,1)} copy(bf16[512,1024]{1,0:T(8,128)(2,1)S(1)} %copy-done) | data formatting | bytes 2097152
  90.0 0.0 copy-done.2
  90.0 0.6 copy.16
Async XLA Ops:
  85.1 2.4 %copy-start.1 = (bf16[512,1024]{1,0:T(8,128)(2,1)S(1)}, bf16[512,1024]{1,0:T(8,128)(2,1)}, u32[]{:S(2)}) copy-start(bf16[512,1024]{1,0:T(8,128)(2,1)} %get-tuple-element.9) | copy-start | bytes 3145732
  87.4 1.6 %copy-start = (bf16[512,1024]{1,0:T(8,128)(2,1)S(1)}, bf16[512,1024]{1,0:T(8,128)(2,1)}, u32[]{:S(2)}) copy-start(bf16[512,1024]{1,0:T(8,128)(2,1)} %get-tuple-element.10) | copy-start | bytes 3145732
  89.0 1.0 %copy-start.2 = (f32[8,512]{1,0:T(8,128)S(1)}, f32[8,512]{1,0:T(8,128)}, u32[]{:S(2)}) copy-start(f32[8,512]{1,0:T(8,128)} %get-tuple-element.11) | copy-start | bytes 49156

commit v2 on v1

--- a/solution.py
+++ b/solution.py
@@ -32,10 +32,10 @@
 def kernel(
     dims,
     q_hbm, k_hbm, v_hbm, y_hbm, w_hbm,
-    gq_hbm, gk_hbm, gv_hbm, gl_hbm,
+    gq_hbm, gk_hbm, gv_hbm, gl_hbm, ba_hbm,
     Q, K, V, Y, W, BS, FR, LS, IS, TOT, YR, YT, XR, COEF, QC, SC, IN, ER, AD,
-    AL1, AI, RP, BXS, BXR, BYS, BYR, DS, BA, GK, GV, OQ, OK, OV, GACC, GLP, GLR,
-    in_sem, w_sem, out_sem, gl_sem,
+    AL1, AI, RP, BXS, BXR, BYS, BYR, DS, BA, DA, OQ, OK, OV, GACC, GLP, GLR,
+    in_sem, w_sem, out_sem, gl_sem, ba_sem,
     f1s, f1r, fl1, f2s, f2r, fys, fyr, fxs, fxr, f3s, f3r,
     bl1, b2s, b2r, b3s, b3r, bxs, bxr, bys, byr, b4s, b4r, glx,
 ):
@@ -113,23 +113,34 @@
     if nhead == 2:
         greet((1 - hd, g, p))
 
-    def state(i):
-        h = wrap(p + half + i)
+    def state(h):
         in_copy(0, h).wait()
         in_copy(1, h).wait()
         BS[h] = tn(K[h], V[h]).astype(BF16)
 
-    loop(n, state, unroll=2)
-    pl.semaphore_wait(barrier, (n - 1) + (nlo - 1) + (nhi - 1) + (nhead - 1))
 
     def f1(h, src):
         return rc(BS.at[h], FR.at[src], f1s.at[h], f1r.at[src], zdev(h))
 
+    def nth(i):
+        near = half - lax.div(i + 1, 2)
+        return wrap(p + near * (1 - 2 * lax.rem(i, 2)))
+
+    state(nth(0))
+    if n > 2:
+        state(nth(1))
+    pl.semaphore_wait(barrier, (n - 1) + (nlo - 1) + (nhi - 1) + (nhead - 1))
+
     def f1_start(i):
-        f1(wrap(p + half + i), p).start()
-
-    loop(half, f1_start)
-    loop(half - 1, lambda i: f1(wrap(p + 1 + i), p).start())
+        f1(nth(i), p).start()
+
+        @pl.when(i + 2 < n)
+        def _():
+            state(nth(i + 2))
+
+    loop(n - 1, f1_start)
+    if n == 2:
+        state(p)
     fl1_copy = rc(BS, LS.at[:, lev(0), :], fl1.at[0], fl1.at[1], zdev(wrap(p + 1)))
     low0 = bit_of(p, 0) == 0
 
@@ -225,10 +236,14 @@
 
     def f3(way, m, s, head):
         dst = wrap(p + 1) if way == 0 else wrap(p - 1)
-        slot = LS.at[head, lev(ib + m), :]
+        rows_here = part(way) if s == half - 1 else (0, DK)
+        slot = LS.at[head, pl.ds((ib + m) * DK + rows_here[0], rows_here[1]), :]
         return rc(slot, slot, f3s.at[way, m, s], f3r.at[way, m, s], zdev(dst))
 
-    hops = (half, half - 1)
+    hops = half
+
+    def part(way):
+        return (way * (DK // 2), DK // 2)
 
     def on_bit(m, body):
         @pl.when(bit_of(g, m) == 1)
@@ -237,10 +252,10 @@
 
     def f3_step(m, s):
         for way in range(2):
-            if s > 0 and s - 1 < hops[way]:
+            if s > 0:
                 head = wrap(p - s) if way == 0 else wrap(p + s)
                 f3(way, m, s - 1, head).wait_recv()
-            if s < hops[way]:
+            if s < hops:
                 head = wrap(p - s) if way == 0 else wrap(p + s)
                 f3(way, m, s, head).start()
 
@@ -270,6 +285,8 @@
             fx(j, j).wait_recv()
 
     loop(nhi - 1, fx_start)
+    for m in range(lob):
+        on_bit(m, lambda: f3_step(m, 1))
     loop(nhi - 1, fx_wait)
     for m in range(hib):
         on_bit(lob + m, lambda: LS.__setitem__((p, lev(ib + lob + m)), masked_sum(XR, nhi, x, m).astype(BF16)))
@@ -298,12 +315,6 @@
                 f2(b, p, h).wait_recv()
         finish(h)
 
-    def far_send(h):
-        for b in range(1, ib):
-            @pl.when(bit_of(p, b) == 1)
-            def _():
-                b2(b, h, p).start()
-
     finish(p)
     for b in range(1, ib):
         @pl.when(bit_of(p, b) == 1)
@@ -311,42 +322,43 @@
             AI[b - 1, p] = AD[p, b]
 
     for s in range(1, half + 1):
-        for m in range(ob):
+        if s < half:
+            for m in range(lob):
+                on_bit(m, lambda: f3_step(m, s + 1))
+        for m in range(lob, ob):
             on_bit(m, lambda: f3_step(m, s))
         heads = [wrap(p - s)] + ([wrap(p + s)] if s < half else [])
         def both(i):
             h = wrap(p - s + 2 * s * i)
             far(h)
         loop(len(heads), both)
-        for h in heads:
-            far_send(h)
 
     def b3(way, m, s):
-        head = wrap(p + half - s) if way == 0 else wrap(p - (half - 1) + s)
         dst = wrap(p + 1) if way == 0 else wrap(p - 1)
+        some_rows = pl.ds(*(part(way) if s == 0 else (0, DK)))
         return rc(
-            AD.at[head, ib + m], RP.at[way, m, s], b3s.at[way, m, s], b3r.at[way, m, s], zdev(dst)
+            AD.at[chained(way, s), ib + m, some_rows], RP.at[way, m, s, some_rows],
+            b3s.at[way, m, s], b3r.at[way, m, s], zdev(dst),
         )
+
+    def chained(way, s):
+        return wrap(p + half - s) if way == 0 else wrap(p - half + s)
 
     def b3_step(m, s):
         for way in range(2):
-            if s < hops[way]:
-                if s > 0:
-                    b3(way, m, s - 1).wait_recv()
-                    head = wrap(p + half - s) if way == 0 else wrap(p - (half - 1) + s)
-                    AD[head, ib + m] = (
-                        AD[head, ib + m].astype(F32) + RP[way, m, s - 1].astype(F32)
-                    ).astype(BF16)
-                b3(way, m, s).start()
-
-    for m in range(ob):
+            if s > 0:
+                b3(way, m, s - 1).wait_recv()
+                some_rows = pl.ds(*(part(way) if s == 1 else (0, DK)))
+                head = chained(way, s)
+                AD[head, ib + m, some_rows] = (
+                    AD[head, ib + m, some_rows].astype(F32) + RP[way, m, s - 1, some_rows].astype(F32)
+                ).astype(BF16)
+            b3(way, m, s).start()
+
+    for m in reversed(range(ob)):
         on_bit(m, lambda: b3_step(m, 0))
 
     bl1_copy = rc(AD.at[:, 0], AL1, bl1.at[0], bl1.at[1], zdev(wrap(p - 1)))
-
-    @pl.when(bit_of(p, 0) == 1)
-    def _():
-        bl1_copy.start()
 
     def heavy(h):
         error = ER[h]
@@ -365,8 +377,8 @@
             grad = grad + COEF[b + 1] * piece
             GACC[b + 1] += query32 * piece
         OQ[h] = grad.astype(BF16)
-        GK[h] = tn(score_grad, query)
-        GV[h] = tn(SC[h], intra_error)
+        OK[h] = tn(score_grad, query).astype(BF16)
+        OV[h] = tn(SC[h], intra_error).astype(BF16)
 
     per_step = n // (half + 1) if half > 1 else 1
     done = 0
@@ -381,24 +393,35 @@
 
     for s in range(1, half):
         some(per_step)
-        for m in range(ob):
+        for m in reversed(range(ob)):
             on_bit(m, lambda: b3_step(m, s))
+
+    for b in reversed(range(1, ib)):
+        @pl.when(bit_of(p, b) == 1)
+        def _():
+            loop(n - 1, lambda i: b2(b, wrap(p + 1 + i), p).start())
+
+    @pl.when(bit_of(p, 0) == 1)
+    def _():
+        bl1_copy.start()
+
     some(per_step)
 
     def own(m):
-        value = AD[p, ib + m].astype(F32) + RP[0, m, hops[0] - 1].astype(F32)
-        if hops[1] > 0:
-            value = value + RP[1, m, hops[1] - 1].astype(F32)
-        return value
-
-    for m in reversed(range(ob)):
-        def own_wait():
-            for way in range(2):
-                if hops[way] > 0:
-                    b3(way, m, hops[way] - 1).wait_recv()
-            if m >= lob:
-                BXS[m - lob] = own(m).astype(BF16)
-        on_bit(m, own_wait)
+        first, second = RP[0, m, half - 1].astype(F32), RP[1, m, half - 1].astype(F32)
+        if half == 1:
+            top = lax.broadcasted_iota(jnp.int32, (DK, DK), 0) < DK // 2
+            return AD[p, ib + m].astype(F32) + jnp.where(top, first, second)
+        return AD[p, ib + m].astype(F32) + first + second
+
+    def own_wait(m):
+        for way in range(2):
+            b3(way, m, half - 1).wait_recv()
+        if m >= lob:
+            BXS[m - lob] = own(m).astype(BF16)
+
+    for m in reversed(range(lob, ob)):
+        on_bit(m, lambda: own_wait(m))
 
     def bx(m, dst, src):
         return rc(BXS.at[m], BXR.at[src], bxs.at[dst], bxr.at[src], xdev(dst))
@@ -414,6 +437,8 @@
             def _():
                 bx(m, j, x).start()
 
+    for m in range(lob):
+        on_bit(m, lambda: own_wait(m))
     some(1)
 
     for j in range(1, nhi):
@@ -491,7 +516,12 @@
         )
         mine = jnp.where(row == num, sums * scales[num], mine)
     GLP[...] = mine
-    loop(n, lambda h: out_copy(0, h).start())
+
+    def write(h):
+        for a in range(3):
+            out_copy(a, h).start()
+
+    loop(n, write)
     if nhead == 2:
         glx_copy = rc(GLP, GLR, glx.at[0], glx.at[1], (1 - hd, g, p))
         glx_copy.start()
@@ -507,13 +537,11 @@
         def _():
             b4(h, h).wait_recv()
         adjoint = BA[h].astype(F32) + jnp.where(low0, AL1[h].astype(F32), 0.0)
-        low = adjoint.astype(BF16)
-        OK[h] = (GK[h] + nn(V[h], low)).astype(BF16)
-        OV[h] = (GV[h] + nt(K[h], low)).astype(BF16)
-        out_copy(1, h).start()
-        out_copy(2, h).start()
+        DA[h] = adjoint.astype(BF16)
 
     loop(n, last)
+    ba_copy = pltpu.make_async_copy(DA, ba_hbm, ba_sem)
+    ba_copy.start()
 
     if nhead == 2:
         glx_copy.wait_recv()
@@ -556,7 +584,7 @@
     for m in range(ob):
         def chain_sent():
             for way in range(2):
-                for s in range(hops[way]):
+                for s in range(hops):
                     f3(way, m, s, wrap(p - s) if way == 0 else wrap(p + s)).wait_send()
                     b3(way, m, s).wait_send()
         on_bit(m, chain_sent)
@@ -576,6 +604,64 @@
 
     loop(n, written)
     gl_copy.wait()
+    ba_copy.wait()
+
+
+def finish_kernel(
+    n, pq_hbm, pk_hbm, pv_hbm, k_hbm, v_hbm, pl_hbm, a_hbm, gq_hbm, gk_hbm, gv_hbm, gl_hbm,
+    GQ, PK, PV, K, V, GL, A, GK, GV, in_sem, out_sem, a_sem, l_sem,
+):
+    def loop(body):
+        def step(i, c):
+            body(i)
+            return c
+        lax.fori_loop(0, n, step, 0)
+
+    def cols(h):
+        return pl.ds(pl.multiple_of(h * DK, DK), DK)
+
+    ins = ((pq_hbm, GQ), (pk_hbm, PK), (pv_hbm, PV), (k_hbm, K), (v_hbm, V))
+    outs = ((gq_hbm, GQ), (gk_hbm, GK), (gv_hbm, GV))
+
+    def in_copy(a, h):
+        return pltpu.make_async_copy(ins[a][0].at[:, cols(h)], ins[a][1].at[h], in_sem.at[a, h])
+
+    def out_copy(a, h):
+        return pltpu.make_async_copy(outs[a][1].at[h], outs[a][0].at[:, cols(h)], out_sem.at[a, h])
+
+    a_copy = pltpu.make_async_copy(a_hbm, A, a_sem)
+    a_copy.start()
+    l_copy = pltpu.make_async_copy(pl_hbm, GL, l_sem.at[0])
+    l_copy.start()
+
+    def start(h):
+        for a in (4, 1, 3, 2, 0):
+            in_copy(a, h).start()
+
+    loop(start)
+    l_copy.wait()
+    l_out = pltpu.make_async_copy(GL, gl_hbm, l_sem.at[1])
+    l_out.start()
+    a_copy.wait()
+
+    def one(h):
+        for a in (4, 1, 3, 2, 0):
+            in_copy(a, h).wait()
+        out_copy(0, h).start()
+        adjoint = A[h]
+        GK[h] = (PK[h].astype(F32) + nn(V[h], adjoint)).astype(BF16)
+        GV[h] = (PV[h].astype(F32) + nt(K[h], adjoint)).astype(BF16)
+        out_copy(1, h).start()
+        out_copy(2, h).start()
+
+    loop(one)
+
+    def done(h):
+        for a in range(3):
+            out_copy(a, h).wait()
+
+    loop(done)
+    l_out.wait()
 
 
 def on_device(queries, key_rows, value_rows, teacher_out, level_weights):
@@ -615,27 +701,40 @@
         wide(levels, rows, DK), low(n, rows, nb * DK), low(n, rows, rows), wide(n, rows, DK),
         low(n, rows, DK), low(n, nb, *sq),
         low(n, *sq), low(ibx, n, *sq), low(2, ob, half, *sq), low(hib, *sq), low(nhi, *sq),
-        low(lob + 1, *sq), low(nlo, *sq), low(n, *sq), low(n, *sq),
-        wide(n, rows, DK), wide(n, rows, DK), low(n, rows, DK), low(n, rows, DK), low(n, rows, DK),
+        low(lob + 1, *sq), low(nlo, *sq), low(n, *sq), low(n, *sq), low(n, *sq),
+        low(n, rows, DK), low(n, rows, DK), low(n, rows, DK),
         wide(levels, rows, DK), wide(levels, rows), wide(levels, rows),
-        dma((4, n)), dma(()), dma((3, n)), dma(()),
+        dma((4, n)), dma(()), dma((3, n)), dma(()), dma(()),
         dma((n,)), dma((n,)), dma((2,)), dma((ibx, n)), dma((ibx, n)),
         dma((nlo,)), dma((nlo,)), dma((nhi,)), dma((nhi,)), dma((2, ob, half)), dma((2, ob, half)),
         dma((2,)), dma((ibx, n)), dma((ibx, n)), dma((2, ob, half)), dma((2, ob, half)),
         dma((nhi,)), dma((nhi,)), dma((nlo,)), dma((nlo,)), dma((n,)), dma((n,)), dma((2,)),
     ]
     big = jax.ShapeDtypeStruct((rows, width), BF16)
-    return pl.pallas_call(
+    part_q, part_k, part_v, part_l, adjoints = pl.pallas_call(
         functools.partial(kernel, dims),
-        out_shape=(big, big, big, jax.ShapeDtypeStruct((levels, rows), F32)),
+        out_shape=(
+            big, big, big, jax.ShapeDtypeStruct((levels, rows), F32), jax.ShapeDtypeStruct((n, *sq), BF16)
+        ),
         in_specs=[any_spec] * 5,
-        out_specs=[any_spec] * 4,
+        out_specs=[any_spec] * 5,
         scratch_shapes=scratch,
         compiler_params=pltpu.CompilerParams(
             collective_id=0, has_side_effects=True, vmem_limit_bytes=60 * 2**20
         ),
         name="log_linear",
     )(queries, key_rows, value_rows, teacher_out, level_weights)
+    return pl.pallas_call(
+        functools.partial(finish_kernel, n),
+        out_shape=(big, big, big, jax.ShapeDtypeStruct((levels, rows), F32)),
+        in_specs=[any_spec] * 7,
+        out_specs=[any_spec] * 4,
+        scratch_shapes=[low(n, rows, DK) for _ in range(5)]
+        + [wide(levels, rows), low(n, *sq), low(n, rows, DK), low(n, rows, DK)]
+        + [dma((5, n)), dma((3, n)), dma(()), dma((2,))],
+        compiler_params=pltpu.CompilerParams(vmem_limit_bytes=60 * 2**20),
+        name="finish",
+    )(part_q, part_k, part_v, key_rows, value_rows, part_l, adjoints)
 
 
 def solution(mesh):

time: 90.8 us -> 85.4 us (0.941)
  the two profiles are of different devices: /device:TPU:32 before, /device:TPU:30 now
where the time goes in v2:
time: 85.4 us; the launch traced here: 83.9 us
  Pallas kernels  83.1 us (97%)
    pallas_call x1, Pallas kernels, on_device(): pl.pallas_call(functools.partial(kernel, dims), out_shape=(big, big, big,...  78.1 us
    pallas_call x1, Pallas kernels, on_device(): pl.pallas_call(functools.partial(finish_kernel, n), out_shape=(big, big,...  5.02 us

profile of v2, /device:TPU:30, one launch (start us, length us, event | category | flops | bytes accessed | tf_op | source)
XLA Modules:
  0.0 83.9 jit_solution(6587200005168901952)
XLA Ops:
  0.6 78.1 %log_linear.1 = (bf16[512,1024]{1,0:T(8,128)(2,1)}, bf16[512,1024]{1,0:T(8,128)(2,1)}, bf16[512,1024]{1,0:T(8,128)(2,1)}, f32[8,512]{1,0:T(8,128)}, bf16[8,128,128]{2,1,0:T(8,128)(2,1)}) custom-call(bf16[512,1024]{1,0:T(8,128)(2,1)} %q_hbm.1, bf16[512,1024]{1,0:T(8,128)(2,1)} %k_hbm.3, bf16[512,1024]{1,0:T(8,128)(2,1)} %v_hbm.3, bf16[512,1024]{1,0:T(8,128)(2,1)} %y_hbm.1, ...), custom_call_target="tpu_custom_call" | custom-call | tf_op jit(solution)/shard_map/log_linear/pallas_call | solution.py:714
  78.7 5.0 %finish.1 = (bf16[512,1024]{1,0:T(8,128)(2,1)}, bf16[512,1024]{1,0:T(8,128)(2,1)}, bf16[512,1024]{1,0:T(8,128)(2,1)}, f32[8,512]{1,0:T(8,128)}) custom-call(bf16[512,1024]{1,0:T(8,128)(2,1)} %get-tuple-element.9.pq_hbm, bf16[512,1024]{1,0:T(8,128)(2,1)} %get-tuple-element.10.pk_hbm, bf16[512,1024]{1,0:T(8,128)(2,1)} %get-tuple-element.11.pv_hbm, ...), custom_call_target="tpu_custom_call" | custom-call | tf_op jit(solution)/shard_map/finish/pallas_call | solution.py:727

commit v3 on v2

--- a/solution.py
+++ b/solution.py
@@ -396,14 +396,14 @@
         for m in reversed(range(ob)):
             on_bit(m, lambda: b3_step(m, s))
 
-    for b in reversed(range(1, ib)):
-        @pl.when(bit_of(p, b) == 1)
-        def _():
-            loop(n - 1, lambda i: b2(b, wrap(p + 1 + i), p).start())
-
     @pl.when(bit_of(p, 0) == 1)
     def _():
         bl1_copy.start()
+
+    for b in reversed(range(1, ib)):
+        @pl.when(bit_of(p, b) == 1)
+        def _():
+            loop(n - 1, lambda i: b2(b, wrap(p + 1 + i), p).start())
 
     some(per_step)
 

time: 85.4 us -> 87.9 us (1.029); the launches traced: 83.9 us -> 87.8 us
  Pallas kernels: 83.1 us -> 87 us
    pallas_call x1, Pallas kernels: 78.1 us -> 82 us  [on_device(): pl.pallas_call(functools.partial(kernel, dims), out_shape=(big, big, big,...]
where the time goes in v3:
time: 87.9 us; the launch traced here: 87.8 us
  Pallas kernels  87 us (99%)
    pallas_call x1, Pallas kernels, on_device(): pl.pallas_call(functools.partial(kernel, dims), out_shape=(big, big, big,...  82 us
    pallas_call x1, Pallas kernels, on_device(): pl.pallas_call(functools.partial(finish_kernel, n), out_shape=(big, big,...  5.02 us

profile of v3, /device:TPU:30, one launch (start us, length us, event | category | flops | bytes accessed | tf_op | source)
XLA Modules:
  0.0 87.8 jit_solution(1033617749045753043)
XLA Ops:
  0.6 82.0 %log_linear.1 = (bf16[512,1024]{1,0:T(8,128)(2,1)}, bf16[512,1024]{1,0:T(8,128)(2,1)}, bf16[512,1024]{1,0:T(8,128)(2,1)}, f32[8,512]{1,0:T(8,128)}, bf16[8,128,128]{2,1,0:T(8,128)(2,1)}) custom-call(bf16[512,1024]{1,0:T(8,128)(2,1)} %q_hbm.1, bf16[512,1024]{1,0:T(8,128)(2,1)} %k_hbm.3, bf16[512,1024]{1,0:T(8,128)(2,1)} %v_hbm.3, bf16[512,1024]{1,0:T(8,128)(2,1)} %y_hbm.1, ...), custom_call_target="tpu_custom_call" | custom-call | tf_op jit(solution)/shard_map/log_linear/pallas_call | solution.py:714
  82.6 5.0 %finish.1 = (bf16[512,1024]{1,0:T(8,128)(2,1)}, bf16[512,1024]{1,0:T(8,128)(2,1)}, bf16[512,1024]{1,0:T(8,128)(2,1)}, f32[8,512]{1,0:T(8,128)}) custom-call(bf16[512,1024]{1,0:T(8,128)(2,1)} %get-tuple-element.9.pq_hbm, bf16[512,1024]{1,0:T(8,128)(2,1)} %get-tuple-element.10.pk_hbm, bf16[512,1024]{1,0:T(8,128)(2,1)} %get-tuple-element.11.pv_hbm, ...), custom_call_target="tpu_custom_call" | custom-call | tf_op jit(solution)/shard_map/finish/pallas_call | solution.py:727
